TPU v7x, 32 devices: a whole 2x2x4 slice. The times are simulated.
32 devices in a mesh: dp: 4 (over x, core), pipe: 2 (over y), tensor: 4 (over z).
Axes of the slice: x: 2, y: 2, z: 4, core: 2. Of those that a mesh axis runs over, the one named last changes fastest.
Arguments:
- weights: bfloat16 [2816, 1408], P(('dp', 'pipe', 'tensor')), may hold values from -6 to 6
- first_moment: bfloat16 [2816, 1408], P(('dp', 'pipe', 'tensor')), may hold values from -6 to 6
- second_moment: bfloat16 [2816, 1408], P(('dp', 'pipe', 'tensor')), may hold values from 0.049804688 to 5
- row_weight: float32 [1408], replicated, may hold values from -1 to 1
- col_weight: float32 [1408], replicated, may hold values from 1 to 4
Outputs:
- weight_tiles: bfloat16 [2816, 1408], P(('pipe', 'tensor'))
- first_tiles: bfloat16 [2816, 1408], P(('pipe', 'tensor'))
- second_tiles: bfloat16 [2816, 1408], P(('pipe', 'tensor'))
- checksums: float32 [3, 2, 4, 11], P(None, 'pipe', 'tensor')
All inputs are finite; a program needn't handle non-finite values.
Results may differ from a plain program's by a relative error of at most 0.001.
Values may be sent and summed in bfloat16 or wider, within the bound.
A program may use at most 64 MiB of HBM per device.

v0:
```python
import jax
import jax.numpy as jnp
from jax import lax
from jax.sharding import PartitionSpec as P

CHECK_COLS = 128


def for_sending(array):
    return jax.tree.map(lambda a: a.astype(jnp.bfloat16) if a.dtype == jnp.float32 else a, array)


def column_sums(data, row_part, col_weight, col_blocks):
    row_mixed = jnp.dot(
        row_part[None, :], data.astype(jnp.float32), precision=lax.Precision.HIGHEST
    )[0]
    return jnp.sum((row_mixed * col_weight).reshape(col_blocks, -1), axis=1)


def shards(weights, first_moment, second_moment, row_weight, col_weight):
    dp_count = lax.axis_size("dp")
    pipe_count = lax.axis_size("pipe")
    tensor_count = lax.axis_size("tensor")
    shard_rows, width = weights.shape
    dp_section = dp_count // pipe_count
    tile_shards = dp_count // tensor_count
    piece_cols = width // dp_count
    tile_rows = shard_rows * dp_count
    col_blocks = width // CHECK_COLS
    factor = float(tile_rows * CHECK_COLS) ** (-0.5)
    sources = (weights, first_moment, second_moment)
    exchanged = (
        lax.all_to_all(sources[0], "dp", split_axis=1, concat_axis=0, tiled=True),
        lax.all_to_all(sources[1], "dp", split_axis=1, concat_axis=0, tiled=True),
        lax.all_to_all(sources[2], "dp", split_axis=1, concat_axis=0, tiled=True),
    )
    grouped = tuple(
        (item.reshape(pipe_count, dp_section, shard_rows, piece_cols) for item in exchanged)
    )
    sectioned = jax.tree.map(
        lambda part, own: part.astype(own.dtype),
        lax.all_to_all(for_sending(grouped), "pipe", split_axis=0, concat_axis=2, tiled=True),
        grouped,
    )
    routed = tuple(
        (item.reshape(tensor_count, tile_shards, 1, shard_rows, piece_cols) for item in sectioned)
    )
    arrived = jax.tree.map(
        lambda part, own: part.astype(own.dtype),
        lax.all_to_all(for_sending(routed), "tensor", split_axis=0, concat_axis=2, tiled=True),
        routed,
    )
    flat_pieces = tuple((item.reshape(tile_rows, piece_cols) for item in arrived))
    tiles = jax.tree.map(
        lambda part, own: part.astype(own.dtype),
        lax.all_gather(for_sending(flat_pieces), "dp", axis=1, tiled=True),
        flat_pieces,
    )
    tensor_pos = lax.axis_index("tensor")
    flat_index = (
        lax.axis_index("dp") * pipe_count + lax.axis_index("pipe")
    ) * tensor_count + tensor_pos
    in_section = flat_index % (dp_count * tensor_count)
    section_of = flat_index // (dp_count * tensor_count)
    tile_of = in_section // dp_count
    row_part = lax.dynamic_slice_in_dim(row_weight, in_section * shard_rows, shard_rows)
    partial_value = jnp.stack(
        [column_sums(item, row_part, col_weight, col_blocks) for item in sources]
    )
    section_hit = (jnp.arange(pipe_count) == section_of).astype(jnp.float32)
    tile_hit = (jnp.arange(tensor_count) == tile_of).astype(jnp.float32)
    spread = (
        partial_value[:, None, None, :]
        * section_hit[None, :, None, None]
        * tile_hit[None, None, :, None]
    )
    summed = lax.psum(spread, ("dp", "pipe", "tensor"))
    checks = (
        lax.dynamic_slice(summed, (0, lax.axis_index("pipe"), tensor_pos, 0), (3, 1, 1, col_blocks))
        * factor
    )
    return (tiles[0], tiles[1], tiles[2], checks)


def solution(mesh):
    return jax.shard_map(
        shards,
        mesh=mesh,
        in_specs=(
            P(("dp", "pipe", "tensor"), None),
            P(("dp", "pipe", "tensor"), None),
            P(("dp", "pipe", "tensor"), None),
            P(),
            P(),
        ),
        out_specs=(
            P(("pipe", "tensor"), None),
            P(("pipe", "tensor"), None),
            P(("pipe", "tensor"), None),
            P(None, "pipe", "tensor", None),
        ),
        check_vma=False,
    )
```

profile of v0, /device:TPU:0, one launch (start us, length us, event | category | flops | bytes accessed | tf_op | source)
XLA Modules:
  0.0 154.1 jit_solution(8427268718347811385)
XLA Ops:
  0.7 1.3 all_to_all.90
  1.9 0.7 copy.33
  2.7 4.4 %all-to-all-start = ((bf16[88,4,352]{2,0,1:T(8,128)(2,1)}), bf16[88,4,352]{2,0,1:T(8,128)(2,1)}, u32[]{:S(2)}, u32[]{:S(2)}) async-start(bf16[88,4,352]{2,0,1:T(8,128)(2,1)} %copy.33), calls=%async_computation | async-start | bytes 540672 | tf_op jit(solution)/shard_map/all_to_all | solution.py:33
  8.1 5.6 %all-to-all-done = bf16[88,4,352]{2,0,1:T(8,128)(2,1)} async-done(((bf16[88,4,352]{2,0,1:T(8,128)(2,1)}), bf16[88,4,352]{2,0,1:T(8,128)(2,1)}, u32[]{:S(2)}, u32[]{:S(2)}) %all-to-all-start) | async-done | bytes 247840 | tf_op jit(solution)/shard_map/all_to_all | solution.py:33
  13.7 4.1 %all-to-all-start.3 = ((bf16[88,4,352]{2,0,1:T(8,128)(2,1)}), bf16[88,4,352]{2,0,1:T(8,128)(2,1)}, u32[]{:S(2)}, u32[]{:S(2)}) async-start(bf16[88,4,352]{2,0,1:T(8,128)(2,1)} %copy.37), calls=%async_computation.3 | async-start | bytes 540672 | tf_op jit(solution)/shard_map/all_to_all | solution.py:34
  18.9 5.1 %all-to-all-done.3 = bf16[88,4,352]{2,0,1:T(8,128)(2,1)} async-done(((bf16[88,4,352]{2,0,1:T(8,128)(2,1)}), bf16[88,4,352]{2,0,1:T(8,128)(2,1)}, u32[]{:S(2)}, u32[]{:S(2)}) %all-to-all-start.3) | async-done | bytes 247840 | tf_op jit(solution)/shard_map/all_to_all | solution.py:34
  24.0 4.1 %all-to-all-start.6 = ((bf16[88,4,352]{2,0,1:T(8,128)(2,1)}), bf16[88,4,352]{2,0,1:T(8,128)(2,1)}, u32[]{:S(2)}, u32[]{:S(2)}) async-start(bf16[88,4,352]{2,0,1:T(8,128)(2,1)} %copy.41), calls=%async_computation.6 | async-start | bytes 540672 | tf_op jit(solution)/shard_map/all_to_all | solution.py:35
  28.7 5.5 %all-to-all-done.6 = bf16[88,4,352]{2,0,1:T(8,128)(2,1)} async-done(((bf16[88,4,352]{2,0,1:T(8,128)(2,1)}), bf16[88,4,352]{2,0,1:T(8,128)(2,1)}, u32[]{:S(2)}, u32[]{:S(2)}) %all-to-all-start.6) | async-done | bytes 247840 | tf_op jit(solution)/shard_map/all_to_all | solution.py:35
  34.2 3.6 %all-to-all-start.1 = ((bf16[2,2,88,352]{3,2,1,0:T(8,128)(2,1)}), bf16[2,2,88,352]{3,2,1,0:T(8,128)(2,1)S(1)}, u32[]{:S(2)}, u32[]{:S(2)}) async-start(bf16[2,2,88,352]{3,2,1,0:T(8,128)(2,1)} %bitcast.1), calls=%async_computation.1 | async-start | bytes 540672 | tf_op jit(solution)/shard_map/all_to_all | solution.py:42
  38.3 5.2 %all-to-all-done.1 = bf16[2,2,88,352]{3,2,1,0:T(8,128)(2,1)S(1)} async-done(((bf16[2,2,88,352]{3,2,1,0:T(8,128)(2,1)}), bf16[2,2,88,352]{3,2,1,0:T(8,128)(2,1)S(1)}, u32[]{:S(2)}, u32[]{:S(2)}) %all-to-all-start.1) | async-done | bytes 247840 | tf_op jit(solution)/shard_map/all_to_all | solution.py:42
  43.5 3.4 %all-to-all-start.4 = ((bf16[2,2,88,352]{3,2,1,0:T(8,128)(2,1)}), bf16[2,2,88,352]{3,2,1,0:T(8,128)(2,1)S(1)}, u32[]{:S(2)}, u32[]{:S(2)}) async-start(bf16[2,2,88,352]{3,2,1,0:T(8,128)(2,1)} %bitcast.8), calls=%async_computation.4 | async-start | bytes 540672 | tf_op jit(solution)/shard_map/all_to_all | solution.py:42
  47.0 5.2 %all-to-all-done.4 = bf16[2,2,88,352]{3,2,1,0:T(8,128)(2,1)S(1)} async-done(((bf16[2,2,88,352]{3,2,1,0:T(8,128)(2,1)}), bf16[2,2,88,352]{3,2,1,0:T(8,128)(2,1)S(1)}, u32[]{:S(2)}, u32[]{:S(2)}) %all-to-all-start.4) | async-done | bytes 247840 | tf_op jit(solution)/shard_map/all_to_all | solution.py:42
  52.1 3.4 %all-to-all-start.7 = ((bf16[2,2,88,352]{3,2,1,0:T(8,128)(2,1)}), bf16[2,2,88,352]{3,2,1,0:T(8,128)(2,1)S(1)}, u32[]{:S(2)}, u32[]{:S(2)}) async-start(bf16[2,2,88,352]{3,2,1,0:T(8,128)(2,1)} %bitcast.15), calls=%async_computation.7 | async-start | bytes 540672 | tf_op jit(solution)/shard_map/all_to_all | solution.py:42
  56.4 4.4 %all-to-all-done.7 = bf16[2,2,88,352]{3,2,1,0:T(8,128)(2,1)S(1)} async-done(((bf16[2,2,88,352]{3,2,1,0:T(8,128)(2,1)}), bf16[2,2,88,352]{3,2,1,0:T(8,128)(2,1)S(1)}, u32[]{:S(2)}, u32[]{:S(2)}) %all-to-all-start.7) | async-done | bytes 247840 | tf_op jit(solution)/shard_map/all_to_all | solution.py:42
  60.8 5.1 %all-to-all-start.2 = ((bf16[4,1,1,88,352]{4,3,2,1,0:T(8,128)(2,1)}), bf16[4,1,1,88,352]{4,3,2,1,0:T(8,128)(2,1)S(1)}, u32[]{:S(2)}, u32[]{:S(2)}) async-start(bf16[4,1,1,88,352]{4,3,2,1,0:T(8,128)(2,1)} %bitcast.5), calls=%async_computation.2 | async-start | bytes 540672 | tf_op jit(solution)/shard_map/all_to_all | solution.py:50
  65.9 39.9 %psum.7 = f32[3,2,4,11]{3,2,1,0:T(4,128)S(1)} all-reduce(f32[3,2,4,11]{3,2,1,0:T(4,128)S(1)} %broadcast_multiply_fusion), channel_id=1, replica_groups=mesh['dp'=4,'pipe'=2,'tensor'=4] {'dp','pipe','tensor'}, use_global_device_ids=true, to_apply=%region_3.4 | all-reduce | flops 264 | bytes 2112 | tf_op jit(solution)/shard_map/psum | solution.py:77
  107.9 3.6 %all-to-all-start.5 = ((bf16[4,1,1,88,352]{4,3,2,1,0:T(8,128)(2,1)}), bf16[4,1,1,88,352]{4,3,2,1,0:T(8,128)(2,1)S(1)}, u32[]{:S(2)}, u32[]{:S(2)}) async-start(bf16[4,1,1,88,352]{4,3,2,1,0:T(8,128)(2,1)} %bitcast.12), calls=%async_computation.5 | async-start | bytes 540672 | tf_op jit(solution)/shard_map/all_to_all | solution.py:50
  111.6 11.0 %all_gather.9 = bf16[352,1408]{0,1:T(8,128)(2,1)S(1)} all-gather(bf16[352,352]{0,1:T(8,128)(2,1)S(1)} %copy.36), channel_id=1, replica_groups=mesh['dp'=4,'pipe'=2,'tensor'=4] {'dp'}, dimensions={1}, use_global_device_ids=true | all-gather | bytes 1239040 | tf_op jit(solution)/shard_map/all_gather | solution.py:56
  122.6 1.9 %copy.45 = bf16[352,1408]{1,0:T(8,128)(2,1)} copy(bf16[352,1408]{0,1:T(8,128)(2,1)S(1)} %all_gather.9) | data formatting | bytes 1982464
  124.5 5.1 %all-to-all-start.8 = ((bf16[4,1,1,88,352]{4,3,2,1,0:T(8,128)(2,1)}), bf16[4,1,1,88,352]{4,3,2,1,0:T(8,128)(2,1)S(1)}, u32[]{:S(2)}, u32[]{:S(2)}) async-start(bf16[4,1,1,88,352]{4,3,2,1,0:T(8,128)(2,1)} %bitcast.19), calls=%async_computation.8 | async-start | bytes 540672 | tf_op jit(solution)/shard_map/all_to_all | solution.py:50
  129.8 10.0 %all_gather.10 = bf16[352,1408]{0,1:T(8,128)(2,1)S(1)} all-gather(bf16[352,352]{0,1:T(8,128)(2,1)S(1)} %copy.40), channel_id=1, replica_groups=mesh['dp'=4,'pipe'=2,'tensor'=4] {'dp'}, dimensions={1}, use_global_device_ids=true | all-gather | bytes 1239040 | tf_op jit(solution)/shard_map/all_gather | solution.py:56
  139.8 1.9 %copy.46 = bf16[352,1408]{1,0:T(8,128)(2,1)} copy(bf16[352,1408]{0,1:T(8,128)(2,1)S(1)} %all_gather.10) | data formatting | bytes 1982464
  141.9 10.3 %all_gather.11 = bf16[352,1408]{0,1:T(8,128)(2,1)S(1)} all-gather(bf16[352,352]{0,1:T(8,128)(2,1)S(1)} %copy.44), channel_id=1, replica_groups=mesh['dp'=4,'pipe'=2,'tensor'=4] {'dp'}, dimensions={1}, use_global_device_ids=true | all-gather | bytes 1239040 | tf_op jit(solution)/shard_map/all_gather | solution.py:56
  152.2 1.9 %copy.47 = bf16[352,1408]{1,0:T(8,128)(2,1)} copy(bf16[352,1408]{0,1:T(8,128)(2,1)S(1)} %all_gather.11) | data formatting | bytes 1982464
  (33 shorter events, 6.7 us)
Async XLA Ops:
  0.6 27.4 %copy-start = (f32[1408]{0:T(1024)S(1)}, f32[1408]{0:T(1024)}, u32[]{:S(2)}) copy-start(f32[1408]{0:T(1024)} %param.8) | copy-start | bytes 16900
  0.6 6.4 %copy-start.3 = (bf16[88,1408]{1,0:T(8,128)(2,1)S(1)}, bf16[88,1408]{1,0:T(8,128)(2,1)}, u32[]{:S(2)}) copy-start(bf16[88,1408]{1,0:T(8,128)(2,1)} %param.6) | copy-start | bytes 743428
  2.7 15.2 %copy-start.2 = (bf16[88,1408]{1,0:T(8,128)(2,1)S(1)}, bf16[88,1408]{1,0:T(8,128)(2,1)}, u32[]{:S(2)}) copy-start(bf16[88,1408]{1,0:T(8,128)(2,1)} %param.7) | copy-start | bytes 743428
  2.7 11.0 %all-to-all-start = ((bf16[88,4,352]{2,0,1:T(8,128)(2,1)}), bf16[88,4,352]{2,0,1:T(8,128)(2,1)}, u32[]{:S(2)}, u32[]{:S(2)}) async-start(bf16[88,4,352]{2,0,1:T(8,128)(2,1)} %copy.33), calls=%async_computation | async-start | bytes 540672 | tf_op jit(solution)/shard_map/all_to_all | solution.py:33
  8.1 20.0 %copy-start.1 = (bf16[88,1408]{1,0:T(8,128)(2,1)S(1)}, bf16[88,1408]{1,0:T(8,128)(2,1)}, u32[]{:S(2)}) copy-start(bf16[88,1408]{1,0:T(8,128)(2,1)} %param.5) | copy-start | bytes 743428
  13.7 10.2 %all-to-all-start.3 = ((bf16[88,4,352]{2,0,1:T(8,128)(2,1)}), bf16[88,4,352]{2,0,1:T(8,128)(2,1)}, u32[]{:S(2)}, u32[]{:S(2)}) async-start(bf16[88,4,352]{2,0,1:T(8,128)(2,1)} %copy.37), calls=%async_computation.3 | async-start | bytes 540672 | tf_op jit(solution)/shard_map/all_to_all | solution.py:34
  18.1 20.0 %copy-start.4 = (f32[1408]{0:T(1024)S(1)}, f32[1408]{0:T(1024)}, u32[]{:S(2)}) copy-start(f32[1408]{0:T(1024)} %param.9) | copy-start | bytes 16900
  24.0 10.2 %all-to-all-start.6 = ((bf16[88,4,352]{2,0,1:T(8,128)(2,1)}), bf16[88,4,352]{2,0,1:T(8,128)(2,1)}, u32[]{:S(2)}, u32[]{:S(2)}) async-start(bf16[88,4,352]{2,0,1:T(8,128)(2,1)} %copy.41), calls=%async_computation.6 | async-start | bytes 540672 | tf_op jit(solution)/shard_map/all_to_all | solution.py:35
  34.2 9.3 %all-to-all-start.1 = ((bf16[2,2,88,352]{3,2,1,0:T(8,128)(2,1)}), bf16[2,2,88,352]{3,2,1,0:T(8,128)(2,1)S(1)}, u32[]{:S(2)}, u32[]{:S(2)}) async-start(bf16[2,2,88,352]{3,2,1,0:T(8,128)(2,1)} %bitcast.1), calls=%async_computation.1 | async-start | bytes 540672 | tf_op jit(solution)/shard_map/all_to_all | solution.py:42
  43.5 8.7 %all-to-all-start.4 = ((bf16[2,2,88,352]{3,2,1,0:T(8,128)(2,1)}), bf16[2,2,88,352]{3,2,1,0:T(8,128)(2,1)S(1)}, u32[]{:S(2)}, u32[]{:S(2)}) async-start(bf16[2,2,88,352]{3,2,1,0:T(8,128)(2,1)} %bitcast.8), calls=%async_computation.4 | async-start | bytes 540672 | tf_op jit(solution)/shard_map/all_to_all | solution.py:42
  52.1 8.7 %all-to-all-start.7 = ((bf16[2,2,88,352]{3,2,1,0:T(8,128)(2,1)}), bf16[2,2,88,352]{3,2,1,0:T(8,128)(2,1)S(1)}, u32[]{:S(2)}, u32[]{:S(2)}) async-start(bf16[2,2,88,352]{3,2,1,0:T(8,128)(2,1)} %bitcast.15), calls=%async_computation.7 | async-start | bytes 540672 | tf_op jit(solution)/shard_map/all_to_all | solution.py:42
  60.8 47.1 %all-to-all-start.2 = ((bf16[4,1,1,88,352]{4,3,2,1,0:T(8,128)(2,1)}), bf16[4,1,1,88,352]{4,3,2,1,0:T(8,128)(2,1)S(1)}, u32[]{:S(2)}, u32[]{:S(2)}) async-start(bf16[4,1,1,88,352]{4,3,2,1,0:T(8,128)(2,1)} %bitcast.5), calls=%async_computation.2 | async-start | bytes 540672 | tf_op jit(solution)/shard_map/all_to_all | solution.py:50
  107.9 16.6 %all-to-all-start.5 = ((bf16[4,1,1,88,352]{4,3,2,1,0:T(8,128)(2,1)}), bf16[4,1,1,88,352]{4,3,2,1,0:T(8,128)(2,1)S(1)}, u32[]{:S(2)}, u32[]{:S(2)}) async-start(bf16[4,1,1,88,352]{4,3,2,1,0:T(8,128)(2,1)} %bitcast.12), calls=%async_computation.5 | async-start | bytes 540672 | tf_op jit(solution)/shard_map/all_to_all | solution.py:50
  124.5 17.2 %all-to-all-start.8 = ((bf16[4,1,1,88,352]{4,3,2,1,0:T(8,128)(2,1)}), bf16[4,1,1,88,352]{4,3,2,1,0:T(8,128)(2,1)S(1)}, u32[]{:S(2)}, u32[]{:S(2)}) async-start(bf16[4,1,1,88,352]{4,3,2,1,0:T(8,128)(2,1)} %bitcast.19), calls=%async_computation.8 | async-start | bytes 540672 | tf_op jit(solution)/shard_map/all_to_all | solution.py:50
where the time goes:
time: 155 us; the launch traced here: 154 us
  blocking collectives  71.2 us (46%)
  starting transfers between devices  36.7 us (24%)
  waiting for transfers between devices  31 us (20%)
  local copies, waits for them, and re-layouts  12.5 us (8%)
    psum x1, blocking collectives, shards(): summed = lax.psum(spread, ('dp', 'pipe', 'tensor'))  39.9 us
    all_gather x3, blocking collectives, shards(): lax.all_gather(for_sending(flat_pieces), 'dp', axis=1, tiled=True)  31.3 us
    all_to_all x3, waiting for transfers between devices, shards(): lax.all_to_all(for_sending(grouped), 'pipe', split_axis=0, concat_axis=2,...  14.7 us
    all_to_all x3, starting transfers between devices, shards(): lax.all_to_all(for_sending(routed), 'tensor', split_axis=0, concat_axis=2...  13.7 us
    all_to_all x3, starting transfers between devices, shards(): lax.all_to_all(for_sending(grouped), 'pipe', split_axis=0, concat_axis=2,...  10.5 us
    unnamed x13, local copies, waits for them, and re-layouts  5.65 us
    all_to_all x1, waiting for transfers between devices, shards(): lax.all_to_all(sources[0], 'dp', split_axis=1, concat_axis=0, tiled=True)  5.65 us
    all_to_all x1, waiting for transfers between devices, shards(): lax.all_to_all(sources[2], 'dp', split_axis=1, concat_axis=0, tiled=True)  5.51 us
  transfers between devices with their start and end apart: 9, of which 6 were waited for; matrix products, arithmetic and copies ran while one was open for 6% of the time, Pallas kernels for 0%

commit v1 on v0

--- a/solution.py
+++ b/solution.py
@@ -74,7 +74,7 @@
         * section_hit[None, :, None, None]
         * tile_hit[None, None, :, None]
     )
-    summed = lax.psum(spread, ("dp", "pipe", "tensor"))
+    summed = jnp.sum(lax.all_gather(spread, ("dp", "pipe", "tensor")), axis=0)
     checks = (
         lax.dynamic_slice(summed, (0, lax.axis_index("pipe"), tensor_pos, 0), (3, 1, 1, col_blocks))
         * factor

time: 155 us -> 183 us (1.18)
  blocking collectives: 71.2 us -> 98.8 us
    all_gather x0 -> x1, blocking collectives: none -> 68.7 us  [shards(): summed = jnp.sum(lax.all_gather(spread, ('dp', 'pipe', 'tensor')), axis=0)]
    psum x1 -> x0, blocking collectives: 39.9 us -> none  [shards(): summed = lax.psum(spread, ('dp', 'pipe', 'tensor'))]
  transfers between devices with their start and end apart: 9 -> 9, of which waited for: 6 -> 6; matrix products, arithmetic and copies ran while one was open for 6% -> 5% of each run, Pallas kernels for 0% -> 0%
where the time goes in v1:
time: 183 us; the launch traced here: 182 us
  blocking collectives  98.8 us (54%)
  starting transfers between devices  36.6 us (20%)
  waiting for transfers between devices  31 us (17%)
  local copies, waits for them, and re-layouts  12.5 us (7%)
    all_gather x1, blocking collectives, shards(): summed = jnp.sum(lax.all_gather(spread, ('dp', 'pipe', 'tensor')), axis=0)  68.7 us
    all_gather x3, blocking collectives, shards(): lax.all_gather(for_sending(flat_pieces), 'dp', axis=1, tiled=True)  30.1 us
    all_to_all x3, waiting for transfers between devices, shards(): lax.all_to_all(for_sending(grouped), 'pipe', split_axis=0, concat_axis=2,...  14.7 us
    all_to_all x3, starting transfers between devices, shards(): lax.all_to_all(for_sending(routed), 'tensor', split_axis=0, concat_axis=2...  13.6 us
    all_to_all x3, starting transfers between devices, shards(): lax.all_to_all(for_sending(grouped), 'pipe', split_axis=0, concat_axis=2,...  10.5 us
    unnamed x13, local copies, waits for them, and re-layouts  5.65 us
    all_to_all x1, waiting for transfers between devices, shards(): lax.all_to_all(sources[0], 'dp', split_axis=1, concat_axis=0, tiled=True)  5.65 us
    all_to_all x1, waiting for transfers between devices, shards(): lax.all_to_all(sources[2], 'dp', split_axis=1, concat_axis=0, tiled=True)  5.51 us
  transfers between devices with their start and end apart: 9, of which 6 were waited for; matrix products, arithmetic and copies ran while one was open for 5% of the time, Pallas kernels for 0%

profile of v1, /device:TPU:0, one launch (start us, length us, event | category | flops | bytes accessed | tf_op | source)
XLA Modules:
  0.0 181.7 jit_solution(5992815658888185025)
XLA Ops:
  0.7 1.3 all_to_all.90
  1.9 0.7 copy.33
  2.7 4.4 %all-to-all-start = ((bf16[88,4,352]{2,0,1:T(8,128)(2,1)}), bf16[88,4,352]{2,0,1:T(8,128)(2,1)}, u32[]{:S(2)}, u32[]{:S(2)}) async-start(bf16[88,4,352]{2,0,1:T(8,128)(2,1)} %copy.33), calls=%async_computation | async-start | bytes 540672 | tf_op jit(solution)/shard_map/all_to_all | solution.py:33
  8.1 5.6 %all-to-all-done = bf16[88,4,352]{2,0,1:T(8,128)(2,1)} async-done(((bf16[88,4,352]{2,0,1:T(8,128)(2,1)}), bf16[88,4,352]{2,0,1:T(8,128)(2,1)}, u32[]{:S(2)}, u32[]{:S(2)}) %all-to-all-start) | async-done | bytes 247840 | tf_op jit(solution)/shard_map/all_to_all | solution.py:33
  13.7 4.1 %all-to-all-start.3 = ((bf16[88,4,352]{2,0,1:T(8,128)(2,1)}), bf16[88,4,352]{2,0,1:T(8,128)(2,1)}, u32[]{:S(2)}, u32[]{:S(2)}) async-start(bf16[88,4,352]{2,0,1:T(8,128)(2,1)} %copy.37), calls=%async_computation.3 | async-start | bytes 540672 | tf_op jit(solution)/shard_map/all_to_all | solution.py:34
  18.9 5.1 %all-to-all-done.3 = bf16[88,4,352]{2,0,1:T(8,128)(2,1)} async-done(((bf16[88,4,352]{2,0,1:T(8,128)(2,1)}), bf16[88,4,352]{2,0,1:T(8,128)(2,1)}, u32[]{:S(2)}, u32[]{:S(2)}) %all-to-all-start.3) | async-done | bytes 247840 | tf_op jit(solution)/shard_map/all_to_all | solution.py:34
  24.0 4.1 %all-to-all-start.6 = ((bf16[88,4,352]{2,0,1:T(8,128)(2,1)}), bf16[88,4,352]{2,0,1:T(8,128)(2,1)}, u32[]{:S(2)}, u32[]{:S(2)}) async-start(bf16[88,4,352]{2,0,1:T(8,128)(2,1)} %copy.41), calls=%async_computation.6 | async-start | bytes 540672 | tf_op jit(solution)/shard_map/all_to_all | solution.py:35
  28.7 5.5 %all-to-all-done.6 = bf16[88,4,352]{2,0,1:T(8,128)(2,1)} async-done(((bf16[88,4,352]{2,0,1:T(8,128)(2,1)}), bf16[88,4,352]{2,0,1:T(8,128)(2,1)}, u32[]{:S(2)}, u32[]{:S(2)}) %all-to-all-start.6) | async-done | bytes 247840 | tf_op jit(solution)/shard_map/all_to_all | solution.py:35
  34.2 3.6 %all-to-all-start.1 = ((bf16[2,2,88,352]{3,2,1,0:T(8,128)(2,1)}), bf16[2,2,88,352]{3,2,1,0:T(8,128)(2,1)S(1)}, u32[]{:S(2)}, u32[]{:S(2)}) async-start(bf16[2,2,88,352]{3,2,1,0:T(8,128)(2,1)} %bitcast.1), calls=%async_computation.1 | async-start | bytes 540672 | tf_op jit(solution)/shard_map/all_to_all | solution.py:42
  38.3 5.2 %all-to-all-done.1 = bf16[2,2,88,352]{3,2,1,0:T(8,128)(2,1)S(1)} async-done(((bf16[2,2,88,352]{3,2,1,0:T(8,128)(2,1)}), bf16[2,2,88,352]{3,2,1,0:T(8,128)(2,1)S(1)}, u32[]{:S(2)}, u32[]{:S(2)}) %all-to-all-start.1) | async-done | bytes 247840 | tf_op jit(solution)/shard_map/all_to_all | solution.py:42
  43.5 3.4 %all-to-all-start.4 = ((bf16[2,2,88,352]{3,2,1,0:T(8,128)(2,1)}), bf16[2,2,88,352]{3,2,1,0:T(8,128)(2,1)S(1)}, u32[]{:S(2)}, u32[]{:S(2)}) async-start(bf16[2,2,88,352]{3,2,1,0:T(8,128)(2,1)} %bitcast.8), calls=%async_computation.4 | async-start | bytes 540672 | tf_op jit(solution)/shard_map/all_to_all | solution.py:42
  47.0 5.2 %all-to-all-done.4 = bf16[2,2,88,352]{3,2,1,0:T(8,128)(2,1)S(1)} async-done(((bf16[2,2,88,352]{3,2,1,0:T(8,128)(2,1)}), bf16[2,2,88,352]{3,2,1,0:T(8,128)(2,1)S(1)}, u32[]{:S(2)}, u32[]{:S(2)}) %all-to-all-start.4) | async-done | bytes 247840 | tf_op jit(solution)/shard_map/all_to_all | solution.py:42
  52.1 3.4 %all-to-all-start.7 = ((bf16[2,2,88,352]{3,2,1,0:T(8,128)(2,1)}), bf16[2,2,88,352]{3,2,1,0:T(8,128)(2,1)S(1)}, u32[]{:S(2)}, u32[]{:S(2)}) async-start(bf16[2,2,88,352]{3,2,1,0:T(8,128)(2,1)} %bitcast.15), calls=%async_computation.7 | async-start | bytes 540672 | tf_op jit(solution)/shard_map/all_to_all | solution.py:42
  56.4 4.4 %all-to-all-done.7 = bf16[2,2,88,352]{3,2,1,0:T(8,128)(2,1)S(1)} async-done(((bf16[2,2,88,352]{3,2,1,0:T(8,128)(2,1)}), bf16[2,2,88,352]{3,2,1,0:T(8,128)(2,1)S(1)}, u32[]{:S(2)}, u32[]{:S(2)}) %all-to-all-start.7) | async-done | bytes 247840 | tf_op jit(solution)/shard_map/all_to_all | solution.py:42
  60.8 5.1 %all-to-all-start.2 = ((bf16[4,1,1,88,352]{4,3,2,1,0:T(8,128)(2,1)}), bf16[4,1,1,88,352]{4,3,2,1,0:T(8,128)(2,1)S(1)}, u32[]{:S(2)}, u32[]{:S(2)}) async-start(bf16[4,1,1,88,352]{4,3,2,1,0:T(8,128)(2,1)} %bitcast.5), calls=%async_computation.2 | async-start | bytes 540672 | tf_op jit(solution)/shard_map/all_to_all | solution.py:50
  65.9 68.7 %all_gather.16 = f32[32,3,2,4,11]{4,3,2,1,0:T(4,128)S(1)} all-gather(f32[1,3,2,4,11]{4,3,2,1,0:T(4,128)S(1)} %broadcast_multiply_fusion), channel_id=1, replica_groups=mesh['dp'=4,'pipe'=2,'tensor'=4] {'dp','pipe','tensor'}, dimensions={0}, use_global_device_ids=true | all-gather | bytes 34848 | tf_op jit(solution)/shard_map/all_gather | solution.py:77
  136.8 3.5 %all-to-all-start.5 = ((bf16[4,1,1,88,352]{4,3,2,1,0:T(8,128)(2,1)}), bf16[4,1,1,88,352]{4,3,2,1,0:T(8,128)(2,1)S(1)}, u32[]{:S(2)}, u32[]{:S(2)}) async-start(bf16[4,1,1,88,352]{4,3,2,1,0:T(8,128)(2,1)} %bitcast.12), calls=%async_computation.5 | async-start | bytes 540672 | tf_op jit(solution)/shard_map/all_to_all | solution.py:50
  140.5 9.8 %all_gather.13 = bf16[352,1408]{0,1:T(8,128)(2,1)S(1)} all-gather(bf16[352,352]{0,1:T(8,128)(2,1)S(1)} %copy.36), channel_id=1, replica_groups=mesh['dp'=4,'pipe'=2,'tensor'=4] {'dp'}, dimensions={1}, use_global_device_ids=true | all-gather | bytes 1239040 | tf_op jit(solution)/shard_map/all_gather | solution.py:56
  150.2 1.9 %copy.45 = bf16[352,1408]{1,0:T(8,128)(2,1)} copy(bf16[352,1408]{0,1:T(8,128)(2,1)S(1)} %all_gather.13) | data formatting | bytes 1982464
  152.1 5.1 %all-to-all-start.8 = ((bf16[4,1,1,88,352]{4,3,2,1,0:T(8,128)(2,1)}), bf16[4,1,1,88,352]{4,3,2,1,0:T(8,128)(2,1)S(1)}, u32[]{:S(2)}, u32[]{:S(2)}) async-start(bf16[4,1,1,88,352]{4,3,2,1,0:T(8,128)(2,1)} %bitcast.19), calls=%async_computation.8 | async-start | bytes 540672 | tf_op jit(solution)/shard_map/all_to_all | solution.py:50
  157.4 10.0 %all_gather.14 = bf16[352,1408]{0,1:T(8,128)(2,1)S(1)} all-gather(bf16[352,352]{0,1:T(8,128)(2,1)S(1)} %copy.40), channel_id=1, replica_groups=mesh['dp'=4,'pipe'=2,'tensor'=4] {'dp'}, dimensions={1}, use_global_device_ids=true | all-gather | bytes 1239040 | tf_op jit(solution)/shard_map/all_gather | solution.py:56
  167.4 1.9 %copy.46 = bf16[352,1408]{1,0:T(8,128)(2,1)} copy(bf16[352,1408]{0,1:T(8,128)(2,1)S(1)} %all_gather.14) | data formatting | bytes 1982464
  169.5 10.3 %all_gather.15 = bf16[352,1408]{0,1:T(8,128)(2,1)S(1)} all-gather(bf16[352,352]{0,1:T(8,128)(2,1)S(1)} %copy.44), channel_id=1, replica_groups=mesh['dp'=4,'pipe'=2,'tensor'=4] {'dp'}, dimensions={1}, use_global_device_ids=true | all-gather | bytes 1239040 | tf_op jit(solution)/shard_map/all_gather | solution.py:56
  179.8 1.9 %copy.47 = bf16[352,1408]{1,0:T(8,128)(2,1)} copy(bf16[352,1408]{0,1:T(8,128)(2,1)S(1)} %all_gather.15) | data formatting | bytes 1982464
  (34 shorter events, 6.8 us)
Async XLA Ops:
  0.6 27.4 %copy-start = (f32[1408]{0:T(1024)S(1)}, f32[1408]{0:T(1024)}, u32[]{:S(2)}) copy-start(f32[1408]{0:T(1024)} %param.8) | copy-start | bytes 16900
  0.6 6.4 %copy-start.3 = (bf16[88,1408]{1,0:T(8,128)(2,1)S(1)}, bf16[88,1408]{1,0:T(8,128)(2,1)}, u32[]{:S(2)}) copy-start(bf16[88,1408]{1,0:T(8,128)(2,1)} %param.6) | copy-start | bytes 743428
  2.7 15.2 %copy-start.2 = (bf16[88,1408]{1,0:T(8,128)(2,1)S(1)}, bf16[88,1408]{1,0:T(8,128)(2,1)}, u32[]{:S(2)}) copy-start(bf16[88,1408]{1,0:T(8,128)(2,1)} %param.7) | copy-start | bytes 743428
  2.7 11.0 %all-to-all-start = ((bf16[88,4,352]{2,0,1:T(8,128)(2,1)}), bf16[88,4,352]{2,0,1:T(8,128)(2,1)}, u32[]{:S(2)}, u32[]{:S(2)}) async-start(bf16[88,4,352]{2,0,1:T(8,128)(2,1)} %copy.33), calls=%async_computation | async-start | bytes 540672 | tf_op jit(solution)/shard_map/all_to_all | solution.py:33
  8.1 20.0 %copy-start.1 = (bf16[88,1408]{1,0:T(8,128)(2,1)S(1)}, bf16[88,1408]{1,0:T(8,128)(2,1)}, u32[]{:S(2)}) copy-start(bf16[88,1408]{1,0:T(8,128)(2,1)} %param.5) | copy-start | bytes 743428
  13.7 10.2 %all-to-all-start.3 = ((bf16[88,4,352]{2,0,1:T(8,128)(2,1)}), bf16[88,4,352]{2,0,1:T(8,128)(2,1)}, u32[]{:S(2)}, u32[]{:S(2)}) async-start(bf16[88,4,352]{2,0,1:T(8,128)(2,1)} %copy.37), calls=%async_computation.3 | async-start | bytes 540672 | tf_op jit(solution)/shard_map/all_to_all | solution.py:34
  18.1 20.0 %copy-start.4 = (f32[1408]{0:T(1024)S(1)}, f32[1408]{0:T(1024)}, u32[]{:S(2)}) copy-start(f32[1408]{0:T(1024)} %param.9) | copy-start | bytes 16900
  24.0 10.2 %all-to-all-start.6 = ((bf16[88,4,352]{2,0,1:T(8,128)(2,1)}), bf16[88,4,352]{2,0,1:T(8,128)(2,1)}, u32[]{:S(2)}, u32[]{:S(2)}) async-start(bf16[88,4,352]{2,0,1:T(8,128)(2,1)} %copy.41), calls=%async_computation.6 | async-start | bytes 540672 | tf_op jit(solution)/shard_map/all_to_all | solution.py:35
  34.2 9.3 %all-to-all-start.1 = ((bf16[2,2,88,352]{3,2,1,0:T(8,128)(2,1)}), bf16[2,2,88,352]{3,2,1,0:T(8,128)(2,1)S(1)}, u32[]{:S(2)}, u32[]{:S(2)}) async-start(bf16[2,2,88,352]{3,2,1,0:T(8,128)(2,1)} %bitcast.1), calls=%async_computation.1 | async-start | bytes 540672 | tf_op jit(solution)/shard_map/all_to_all | solution.py:42
  43.5 8.7 %all-to-all-start.4 = ((bf16[2,2,88,352]{3,2,1,0:T(8,128)(2,1)}), bf16[2,2,88,352]{3,2,1,0:T(8,128)(2,1)S(1)}, u32[]{:S(2)}, u32[]{:S(2)}) async-start(bf16[2,2,88,352]{3,2,1,0:T(8,128)(2,1)} %bitcast.8), calls=%async_computation.4 | async-start | bytes 540672 | tf_op jit(solution)/shard_map/all_to_all | solution.py:42
  52.1 8.7 %all-to-all-start.7 = ((bf16[2,2,88,352]{3,2,1,0:T(8,128)(2,1)}), bf16[2,2,88,352]{3,2,1,0:T(8,128)(2,1)S(1)}, u32[]{:S(2)}, u32[]{:S(2)}) async-start(bf16[2,2,88,352]{3,2,1,0:T(8,128)(2,1)} %bitcast.15), calls=%async_computation.7 | async-start | bytes 540672 | tf_op jit(solution)/shard_map/all_to_all | solution.py:42
  60.8 76.0 %all-to-all-start.2 = ((bf16[4,1,1,88,352]{4,3,2,1,0:T(8,128)(2,1)}), bf16[4,1,1,88,352]{4,3,2,1,0:T(8,128)(2,1)S(1)}, u32[]{:S(2)}, u32[]{:S(2)}) async-start(bf16[4,1,1,88,352]{4,3,2,1,0:T(8,128)(2,1)} %bitcast.5), calls=%async_computation.2 | async-start | bytes 540672 | tf_op jit(solution)/shard_map/all_to_all | solution.py:50
  136.8 15.3 %all-to-all-start.5 = ((bf16[4,1,1,88,352]{4,3,2,1,0:T(8,128)(2,1)}), bf16[4,1,1,88,352]{4,3,2,1,0:T(8,128)(2,1)S(1)}, u32[]{:S(2)}, u32[]{:S(2)}) async-start(bf16[4,1,1,88,352]{4,3,2,1,0:T(8,128)(2,1)} %bitcast.12), calls=%async_computation.5 | async-start | bytes 540672 | tf_op jit(solution)/shard_map/all_to_all | solution.py:50
  152.1 17.2 %all-to-all-start.8 = ((bf16[4,1,1,88,352]{4,3,2,1,0:T(8,128)(2,1)}), bf16[4,1,1,88,352]{4,3,2,1,0:T(8,128)(2,1)S(1)}, u32[]{:S(2)}, u32[]{:S(2)}) async-start(bf16[4,1,1,88,352]{4,3,2,1,0:T(8,128)(2,1)} %bitcast.19), calls=%async_computation.8 | async-start | bytes 540672 | tf_op jit(solution)/shard_map/all_to_all | solution.py:50
